TPU v7x, 32 devices: a whole 2x2x4 slice. The times are simulated.
32 devices in a mesh: owner: 4 (over y, core), rows: 8 (over z, x).
Axes of the slice: x: 2, y: 2, z: 4, core: 2. Of those that a mesh axis runs over, the one named last changes fastest.
Arguments:
- train_gate: float32 [128, 2048, 768], P('owner', 'rows'), may hold values from -0.125 to 0.125
- train_up: float32 [128, 2048, 768], P('owner', 'rows'), may hold values from -0.125 to 0.125
- router_weight: float32 [2048, 128], P('rows', 'owner'), may hold values from -0.125 to 0.125
- router_gain: float32 [2048], P('rows'), may hold values from 0.25 to 1.75
Outputs:
- ready_gate: bfloat16 [128, 768, 2048], P(('owner', 'rows'))
- ready_up: bfloat16 [128, 768, 2048], P(('owner', 'rows'))
- serve_router: bfloat16 [2048, 128], replicated
All inputs are finite; a program needn't handle non-finite values.
Results may differ from a plain program's by a relative error of at most 0.001.
Values may be sent and summed in bfloat16 or wider, within the bound.
A program may use at most 192 MiB of HBM per device.

v0:
```python
import jax
import jax.numpy as jnp
from jax import lax
from jax.sharding import PartitionSpec as P


def on_device(train_gate, train_up, router_weight, router_gain):
    narrow_gate, narrow_up = (train_gate.astype(jnp.bfloat16), train_up.astype(jnp.bfloat16))
    ready_gate, ready_up = (
        lax.all_to_all(narrow_gate, "rows", split_axis=0, concat_axis=1, tiled=True),
        lax.all_to_all(narrow_up, "rows", split_axis=0, concat_axis=1, tiled=True),
    )
    ready_gate = jnp.transpose(ready_gate, (0, 2, 1))
    ready_up = jnp.transpose(ready_up, (0, 2, 1))
    part_router = (router_weight * router_gain[:, None]).astype(jnp.bfloat16)
    row_router = lax.all_gather(part_router, "rows", axis=0, tiled=True)
    serve_router = lax.all_gather(row_router, "owner", axis=1, tiled=True)
    return (ready_gate, ready_up, serve_router)


def solution(mesh):
    placed = (P("owner", "rows", None), P("owner", "rows", None), P("rows", "owner"), P("rows"))
    return jax.shard_map(
        on_device,
        mesh=mesh,
        in_specs=placed,
        out_specs=(P(("owner", "rows"), None, None), P(("owner", "rows"), None, None), P()),
        check_vma=False,
    )
```

profile of v0, /device:TPU:0, one launch (start us, length us, event | category | flops | bytes accessed | tf_op | source)
XLA Modules:
  0.0 672.7 jit_solution(13268045616997217038)
XLA Ops:
  0.6 13.2 %convert_element_type.9 = bf16[32,256,768]{2,1,0:T(8,128)(2,1)} convert(f32[32,256,768]{2,1,0:T(8,128)} %param.4) | non-fusion elementwise | flops 6291456 | bytes 37748736 | tf_op jit(solution)/shard_map/convert_element_type | solution.py:8
  13.8 7.3 %all-to-all-start = ((bf16[32,256,768]{2,1,0:T(8,128)(2,1)}), bf16[32,256,768]{2,1,0:T(8,128)(2,1)}, u32[]{:S(2)}, u32[]{:S(2)}) async-start(bf16[32,256,768]{2,1,0:T(8,128)(2,1)} %convert_element_type.9), calls=%async_computation | async-start | bytes 25165824 | tf_op jit(solution)/shard_map/all_to_all | solution.py:10
  21.1 13.4 %convert_element_type.10 = bf16[32,256,768]{2,1,0:T(8,128)(2,1)} convert(f32[32,256,768]{2,1,0:T(8,128)} %param.5) | non-fusion elementwise | flops 6291456 | bytes 37748736 | tf_op jit(solution)/shard_map/convert_element_type | solution.py:8
  34.5 0.0 copy-start
  34.5 0.0 copy-start.1
  34.5 259.7 %all-to-all-done = bf16[32,256,768]{2,1,0:T(8,128)(2,1)} async-done(((bf16[32,256,768]{2,1,0:T(8,128)(2,1)}), bf16[32,256,768]{2,1,0:T(8,128)(2,1)}, u32[]{:S(2)}, u32[]{:S(2)}) %all-to-all-start) | async-done | bytes 12582944 | tf_op jit(solution)/shard_map/all_to_all | solution.py:10
  294.2 5.3 all-to-all-start.1
  299.5 0.0 copy-done
  299.5 0.0 copy-done.1
  299.5 292.2 %all_gather.6 = bf16[2048,32]{0,1:T(8,128)(2,1)S(1)} all-gather(bf16[256,32]{0,1:T(8,128)(2,1)S(1)} %multiply_convert_fusion), channel_id=1, replica_groups=mesh['owner'=4,'rows'=8] {'rows'}, dimensions={0}, use_global_device_ids=true | all-gather | bytes 147456 | tf_op jit(solution)/shard_map/all_gather | solution.py:16
  591.8 7.2 %all_gather.7 = bf16[2048,128]{0,1:T(8,128)(2,1)S(1)} all-gather(bf16[2048,32]{0,1:T(8,128)(2,1)S(1)} %all_gather.6), channel_id=1, replica_groups=mesh['owner'=4,'rows'=8] {'owner'}, dimensions={1}, use_global_device_ids=true | all-gather | bytes 655360 | tf_op jit(solution)/shard_map/all_gather | solution.py:17
  598.9 1.0 copy.12
  599.9 16.9 %copy.10 = bf16[8,4,256,768]{2,0,3,1:T(8,128)(2,1)} copy(bf16[8,4,256,768]{3,2,1,0:T(8,128)(2,1)} %bitcast) | data formatting | bytes 25165824 | tf_op jit(solution)/shard_map/all_to_all | solution.py:10
  616.8 19.5 %all_to_all.29 = bf16[4,2048,768]{1,2,0:T(8,128)(2,1)} reshape(bf16[4,8,256,768]{2,1,3,0:T(8,128)(2,1)} %bitcast.14) | data formatting | bytes 25165824 | tf_op jit(solution)/shard_map/all_to_all | solution.py:10
  636.3 0.0 all-to-all-done.1
  636.3 16.9 %copy.11 = bf16[8,4,256,768]{2,0,3,1:T(8,128)(2,1)} copy(bf16[8,4,256,768]{3,2,1,0:T(8,128)(2,1)} %bitcast.3) | data formatting | bytes 25165824 | tf_op jit(solution)/shard_map/all_to_all | solution.py:11
  653.2 19.5 %all_to_all.33 = bf16[4,2048,768]{1,2,0:T(8,128)(2,1)} reshape(bf16[4,8,256,768]{2,1,3,0:T(8,128)(2,1)} %bitcast.15) | data formatting | bytes 25165824 | tf_op jit(solution)/shard_map/all_to_all | solution.py:11
  (1 shorter events, 0.0 us)
Async XLA Ops:
  13.8 280.3 %all-to-all-start = ((bf16[32,256,768]{2,1,0:T(8,128)(2,1)}), bf16[32,256,768]{2,1,0:T(8,128)(2,1)}, u32[]{:S(2)}, u32[]{:S(2)}) async-start(bf16[32,256,768]{2,1,0:T(8,128)(2,1)} %convert_element_type.9), calls=%async_computation | async-start | bytes 25165824 | tf_op jit(solution)/shard_map/all_to_all | solution.py:10
  34.5 265.0 %copy-start = (f32[256,32]{0,1:T(8,128)S(1)}, f32[256,32]{0,1:T(8,128)}, u32[]{:S(2)}) copy-start(f32[256,32]{0,1:T(8,128)} %param.6) | copy-start | bytes 98308
  34.5 265.0 %copy-start.1 = (f32[256]{0:T(256)S(1)}, f32[256]{0:T(256)}, u32[]{:S(2)}) copy-start(f32[256]{0:T(256)} %param.7) | copy-start | bytes 3076
  294.2 342.1 %all-to-all-start.1 = ((bf16[32,256,768]{2,1,0:T(8,128)(2,1)}), bf16[32,256,768]{2,1,0:T(8,128)(2,1)}, u32[]{:S(2)}, u32[]{:S(2)}) async-start(bf16[32,256,768]{2,1,0:T(8,128)(2,1)} %convert_element_type.10), calls=%async_computation.1 | async-start | bytes 25165824 | tf_op jit(solution)/shard_map/all_to_all | solution.py:11
where the time goes:
time: 675 us; the launch traced here: 673 us
  blocking collectives  299 us (44%)
  waiting for transfers between devices  260 us (39%)
  local copies, waits for them, and re-layouts  73.7 us (11%)
  other arithmetic  26.6 us (4%)
  starting transfers between devices  12.6 us (2%)
    all_gather x1, blocking collectives, on_device(): row_router = lax.all_gather(part_router, 'rows', axis=0, tiled=True)  292 us
    all_to_all x1, waiting for transfers between devices, on_device(): lax.all_to_all(narrow_gate, 'rows', split_axis=0, concat_axis=1, tiled=True)  260 us
    all_to_all x2, local copies, waits for them, and re-layouts, on_device(): lax.all_to_all(narrow_up, 'rows', split_axis=0, concat_axis=1, tiled=True)  36.4 us
    all_to_all x2, local copies, waits for them, and re-layouts, on_device(): lax.all_to_all(narrow_gate, 'rows', split_axis=0, concat_axis=1, tiled=True)  36.3 us
  transfers between devices with their start and end apart: 2, of which 1 were waited for; matrix products, arithmetic and copies ran while one was open for 5% of the time, Pallas kernels for 0%

commit v1 on v0

--- a/solution.py
+++ b/solution.py
@@ -2,6 +2,7 @@
 import jax.numpy as jnp
 from jax import lax
 from jax.sharding import PartitionSpec as P
+from jax.lax import axis_index, axis_size, ppermute
 
 
 def on_device(train_gate, train_up, router_weight, router_gain):
@@ -13,7 +14,28 @@
     ready_gate = jnp.transpose(ready_gate, (0, 2, 1))
     ready_up = jnp.transpose(ready_up, (0, 2, 1))
     part_router = (router_weight * router_gain[:, None]).astype(jnp.bfloat16)
-    row_router = lax.all_gather(part_router, "rows", axis=0, tiled=True)
+    buffers = []
+    n_chips = axis_size("rows")
+    nth = 0
+    while nth < n_chips:
+        buffers.append((nth, (nth + 1) % n_chips))
+        nth += 1
+    grid = []
+    nth = 0
+    while nth < n_chips:
+        grid.append((nth, (nth - 1) % n_chips))
+        nth = nth + 1
+    u_next, arr_now = ([part_router], [part_router])
+    for _ in range(n_chips // 2):
+        u_next.append(ppermute(u_next[-1], "rows", buffers))
+    at = 0
+    while at < (n_chips - 1) // 2:
+        arr_now.append(ppermute(arr_now[-1], "rows", grid))
+        at += 1
+    found_now = jnp.concatenate([*u_next[::-1], *arr_now[1:]], axis=0)
+    row_router = jnp.roll(
+        found_now, (axis_index("rows") - n_chips // 2) * part_router.shape[0], axis=0
+    )
     serve_router = lax.all_gather(row_router, "owner", axis=1, tiled=True)
     return (ready_gate, ready_up, serve_router)
 

time: 675 us -> 668 us (0.990)
  blocking collectives: 299 us -> 7.2 us
  waiting for transfers between devices: 260 us -> 474 us
  starting transfers between devices: 12.6 us -> 80.9 us
    all_gather x1 -> x0, blocking collectives: 292 us -> none  [on_device(): row_router = lax.all_gather(part_router, 'rows', axis=0, tiled=True)]
    ppermute x0 -> x7, waiting for transfers between devices: none -> 214 us  [the longest x4 209 us: on_device(): u_next.append(ppermute(u_next[-1], 'rows', buffers))]
    ppermute x0 -> x7, starting transfers between devices: none -> 68.3 us  [the longest x4 59.4 us: on_device(): u_next.append(ppermute(u_next[-1], 'rows', buffers))]
  transfers between devices with their start and end apart: 2 -> 9, of which waited for: 1 -> 7; matrix products, arithmetic and copies ran while one was open for 5% -> 5% of each run, Pallas kernels for 0% -> 0%
where the time goes in v1:
time: 668 us; the launch traced here: 663 us
  waiting for transfers between devices  474 us (71%)
  starting transfers between devices  80.9 us (12%)
  local copies, waits for them, and re-layouts  73.8 us (11%)
  other arithmetic  26.5 us (4%)
  blocking collectives  7.2 us (1%)
    all_to_all x1, waiting for transfers between devices, on_device(): lax.all_to_all(narrow_gate, 'rows', split_axis=0, concat_axis=1, tiled=True)  260 us
    ppermute x4, waiting for transfers between devices, on_device(): u_next.append(ppermute(u_next[-1], 'rows', buffers))  209 us
    ppermute x4, starting transfers between devices, on_device(): u_next.append(ppermute(u_next[-1], 'rows', buffers))  59.4 us
    all_to_all x2, local copies, waits for them, and re-layouts, on_device(): lax.all_to_all(narrow_up, 'rows', split_axis=0, concat_axis=1, tiled=True)  36.4 us
    all_to_all x2, local copies, waits for them, and re-layouts, on_device(): lax.all_to_all(narrow_gate, 'rows', split_axis=0, concat_axis=1, tiled=True)  36.3 us
  transfers between devices with their start and end apart: 9, of which 7 were waited for; matrix products, arithmetic and copies ran while one was open for 5% of the time, Pallas kernels for 0%

profile of v1, /device:TPU:0, one launch (start us, length us, event | category | flops | bytes accessed | tf_op | source)
XLA Modules:
  0.0 663.0 jit_solution(4247206100921887915)
XLA Ops:
  0.6 13.2 %convert_element_type.9 = bf16[32,256,768]{2,1,0:T(8,128)(2,1)} convert(f32[32,256,768]{2,1,0:T(8,128)} %param.4) | non-fusion elementwise | flops 6291456 | bytes 37748736 | tf_op jit(solution)/shard_map/convert_element_type | solution.py:9
  13.8 7.3 %all-to-all-start = ((bf16[32,256,768]{2,1,0:T(8,128)(2,1)}), bf16[32,256,768]{2,1,0:T(8,128)(2,1)}, u32[]{:S(2)}, u32[]{:S(2)}) async-start(bf16[32,256,768]{2,1,0:T(8,128)(2,1)} %convert_element_type.9), calls=%async_computation | async-start | bytes 25165824 | tf_op jit(solution)/shard_map/all_to_all | solution.py:11
  21.1 13.3 %convert_element_type.10 = bf16[32,256,768]{2,1,0:T(8,128)(2,1)} convert(f32[32,256,768]{2,1,0:T(8,128)} %param.5) | non-fusion elementwise | flops 6291456 | bytes 37748736 | tf_op jit(solution)/shard_map/convert_element_type | solution.py:9
  34.4 0.0 copy-start
  34.4 0.0 copy-start.1
  34.4 259.8 %all-to-all-done = bf16[32,256,768]{2,1,0:T(8,128)(2,1)} async-done(((bf16[32,256,768]{2,1,0:T(8,128)(2,1)}), bf16[32,256,768]{2,1,0:T(8,128)(2,1)}, u32[]{:S(2)}, u32[]{:S(2)}) %all-to-all-start) | async-done | bytes 12582944 | tf_op jit(solution)/shard_map/all_to_all | solution.py:11
  294.2 5.4 all-to-all-start.1
  299.5 0.0 copy-done
  299.5 0.0 copy-done.1
  299.6 1.9 collective-permute-start
  301.5 205.0 %collective-permute-done = bf16[256,32]{0,1:T(8,128)(2,1)S(1)} collective-permute-done((bf16[256,32]{0,1:T(8,128)(2,1)S(1)}, bf16[256,32]{0,1:T(8,128)(2,1)S(1)}, u32[]{:S(2)}, u32[]{:S(2)}) %collective-permute-start) | collective-permute-done | bytes 16416 | tf_op jit(solution)/shard_map/ppermute | solution.py:30
  506.5 0.0 collective-permute-start.1
  506.5 4.7 collective-permute-start.4
  511.2 1.8 collective-permute-done.1
  513.0 24.6 %collective-permute-start.2 = (bf16[256,32]{0,1:T(8,128)(2,1)S(1)}, bf16[256,32]{0,1:T(8,128)(2,1)S(1)}, u32[]{:S(2)}, u32[]{:S(2)}) collective-permute-start(bf16[256,32]{0,1:T(8,128)(2,1)S(1)} %collective-permute-done.1), channel_id=1, source_target_pairs={{0,1},{1,2},{2,3},{3,4},{4,5},{5,6},{6,7},{7,0},{8,9},{9,10},{10,1... | collective-permute-start | bytes 49160 | tf_op jit(solution)/shard_map/ppermute | solution.py:30
  537.6 0.0 collective-permute-done.4
  537.6 4.2 collective-permute-start.5
  541.8 1.7 collective-permute-done.2
  543.5 32.8 %collective-permute-start.3 = (bf16[256,32]{0,1:T(8,128)(2,1)S(1)}, bf16[256,32]{0,1:T(8,128)(2,1)S(1)}, u32[]{:S(2)}, u32[]{:S(2)}) collective-permute-start(bf16[256,32]{0,1:T(8,128)(2,1)S(1)} %collective-permute-done.2), channel_id=1, source_target_pairs={{0,1},{1,2},{2,3},{3,4},{4,5},{5,6},{6,7},{7,0},{8,9},{9,10},{10,1... | collective-permute-start | bytes 49160 | tf_op jit(solution)/shard_map/ppermute | solution.py:30
  576.4 0.5 collective-permute-done.5
  576.9 0.0 collective-permute-start.6
  576.9 0.9 collective-permute-done.3
  577.8 4.1 collective-permute-done.6
  582.1 7.2 %all_gather.3 = bf16[2048,128]{0,1:T(8,128)(2,1)S(1)} all-gather(bf16[2048,32]{0,1:T(8,128)(2,1)S(1)} %constant_dynamic-slice_fusion), channel_id=1, replica_groups=mesh['owner'=4,'rows'=8] {'owner'}, dimensions={1}, use_global_device_ids=true | all-gather | bytes 655360 | tf_op jit(solution)/shard_map/all_gather | solution.py:39
  589.3 1.0 copy.12
  590.3 16.9 %copy.10 = bf16[8,4,256,768]{2,0,3,1:T(8,128)(2,1)} copy(bf16[8,4,256,768]{3,2,1,0:T(8,128)(2,1)} %bitcast) | data formatting | bytes 25165824 | tf_op jit(solution)/shard_map/all_to_all | solution.py:11
  607.2 19.5 %all_to_all.29 = bf16[4,2048,768]{1,2,0:T(8,128)(2,1)} reshape(bf16[4,8,256,768]{2,1,3,0:T(8,128)(2,1)} %bitcast.14) | data formatting | bytes 25165824 | tf_op jit(solution)/shard_map/all_to_all | solution.py:11
  626.6 0.0 all-to-all-done.1
  626.7 16.9 %copy.11 = bf16[8,4,256,768]{2,0,3,1:T(8,128)(2,1)} copy(bf16[8,4,256,768]{3,2,1,0:T(8,128)(2,1)} %bitcast.3) | data formatting | bytes 25165824 | tf_op jit(solution)/shard_map/all_to_all | solution.py:12
  643.5 19.5 %all_to_all.33 = bf16[4,2048,768]{1,2,0:T(8,128)(2,1)} reshape(bf16[4,8,256,768]{2,1,3,0:T(8,128)(2,1)} %bitcast.15) | data formatting | bytes 25165824 | tf_op jit(solution)/shard_map/all_to_all | solution.py:12
  (18 shorter events, 0.1 us)
Async XLA Ops:
  13.8 280.3 %all-to-all-start = ((bf16[32,256,768]{2,1,0:T(8,128)(2,1)}), bf16[32,256,768]{2,1,0:T(8,128)(2,1)}, u32[]{:S(2)}, u32[]{:S(2)}) async-start(bf16[32,256,768]{2,1,0:T(8,128)(2,1)} %convert_element_type.9), calls=%async_computation | async-start | bytes 25165824 | tf_op jit(solution)/shard_map/all_to_all | solution.py:11
  34.4 265.2 %copy-start = (f32[256,32]{0,1:T(8,128)S(1)}, f32[256,32]{0,1:T(8,128)}, u32[]{:S(2)}) copy-start(f32[256,32]{0,1:T(8,128)} %param.6) | copy-start | bytes 98308
  34.4 265.2 %copy-start.1 = (f32[256]{0:T(256)S(1)}, f32[256]{0:T(256)}, u32[]{:S(2)}) copy-start(f32[256]{0:T(256)} %param.7) | copy-start | bytes 3076
  294.2 332.5 %all-to-all-start.1 = ((bf16[32,256,768]{2,1,0:T(8,128)(2,1)}), bf16[32,256,768]{2,1,0:T(8,128)(2,1)}, u32[]{:S(2)}, u32[]{:S(2)}) async-start(bf16[32,256,768]{2,1,0:T(8,128)(2,1)} %convert_element_type.10), calls=%async_computation.1 | async-start | bytes 25165824 | tf_op jit(solution)/shard_map/all_to_all | solution.py:12
  299.6 206.9 %collective-permute-start = (bf16[256,32]{0,1:T(8,128)(2,1)S(1)}, bf16[256,32]{0,1:T(8,128)(2,1)S(1)}, u32[]{:S(2)}, u32[]{:S(2)}) collective-permute-start(bf16[256,32]{0,1:T(8,128)(2,1)S(1)} %multiply_convert_fusion), channel_id=1, source_target_pairs={{0,1},{1,2},{2,3},{3,4},{4,5},{5,6},{6,7},{7,0},{8,9},{9,10},{10,1... | collective-permute-start | bytes 49160 | tf_op jit(solution)/shard_map/ppermute | solution.py:30
  506.5 6.5 collective-permute-start.1
  506.5 31.1 %collective-permute-start.4 = (bf16[256,32]{0,1:T(8,128)(2,1)S(1)}, bf16[256,32]{0,1:T(8,128)(2,1)S(1)}, u32[]{:S(2)}, u32[]{:S(2)}) collective-permute-start(bf16[256,32]{0,1:T(8,128)(2,1)S(1)} %multiply_convert_fusion), channel_id=1, source_target_pairs={{0,7},{1,0},{2,1},{3,2},{4,3},{5,4},{6,5},{7,6},{8,15},{9,8},{10,9... | collective-permute-start | bytes 49160 | tf_op jit(solution)/shard_map/ppermute | solution.py:33
  513.0 30.5 %collective-permute-start.2 = (bf16[256,32]{0,1:T(8,128)(2,1)S(1)}, bf16[256,32]{0,1:T(8,128)(2,1)S(1)}, u32[]{:S(2)}, u32[]{:S(2)}) collective-permute-start(bf16[256,32]{0,1:T(8,128)(2,1)S(1)} %collective-permute-done.1), channel_id=1, source_target_pairs={{0,1},{1,2},{2,3},{3,4},{4,5},{5,6},{6,7},{7,0},{8,9},{9,10},{10,1... | collective-permute-start | bytes 49160 | tf_op jit(solution)/shard_map/ppermute | solution.py:30
  537.6 39.3 %collective-permute-start.5 = (bf16[256,32]{0,1:T(8,128)(2,1)S(1)}, bf16[256,32]{0,1:T(8,128)(2,1)S(1)}, u32[]{:S(2)}, u32[]{:S(2)}) collective-permute-start(bf16[256,32]{0,1:T(8,128)(2,1)S(1)} %collective-permute-done.4), channel_id=1, source_target_pairs={{0,7},{1,0},{2,1},{3,2},{4,3},{5,4},{6,5},{7,6},{8,15},{9,8},{10,9... | collective-permute-start | bytes 49160 | tf_op jit(solution)/shard_map/ppermute | solution.py:33
  543.5 34.3 %collective-permute-start.3 = (bf16[256,32]{0,1:T(8,128)(2,1)S(1)}, bf16[256,32]{0,1:T(8,128)(2,1)S(1)}, u32[]{:S(2)}, u32[]{:S(2)}) collective-permute-start(bf16[256,32]{0,1:T(8,128)(2,1)S(1)} %collective-permute-done.2), channel_id=1, source_target_pairs={{0,1},{1,2},{2,3},{3,4},{4,5},{5,6},{6,7},{7,0},{8,9},{9,10},{10,1... | collective-permute-start | bytes 49160 | tf_op jit(solution)/shard_map/ppermute | solution.py:30
  576.9 5.1 collective-permute-start.6
